TPU v7x, 32 devices: a whole 2x2x4 slice. The times are simulated.
32 devices in a mesh: samp: 8 (over z, x), win: 1, snp: 4 (over y, core).
Axes of the slice: x: 2, y: 2, z: 4, core: 2. Of those that a mesh axis runs over, the one named last changes fastest.
Arguments:
- dosages: bfloat16 [4096, 4096], P('samp', ('win', 'snp')), may hold values from 0 to 2
Outputs:
- r_squared: float32 [1, 4096, 4096], P('win', 'samp', 'snp')
- band_r_squared: float32 [1, 1024, 4096], P('win', 'samp', 'snp')
All inputs are finite; a program needn't handle non-finite values.
Results may differ from a plain program's by a relative error of at most 0.0003.
Values may be sent and summed in bfloat16 or wider, within the bound.
A program may use at most 128 MiB of HBM per device.

v0:
```python
import jax
import jax.numpy as jnp
from jax import lax
from jax.sharding import PartitionSpec as P

OV = 1024


var_floor = 0.05


def passed_along(shard, axis, by):
    devices = lax.axis_size(axis)
    return lax.ppermute(shard, axis, [(i, (i + by) % devices) for i in range(devices)])


def squared_corr(gram, col_sum, col_sq, row_sum, row_sq, count):
    col_mean = col_sum / count
    row_mean = row_sum / count
    col_var = jnp.maximum(col_sq / count - col_mean * col_mean, var_floor)
    row_var = jnp.maximum(row_sq / count - row_mean * row_mean, var_floor)
    covar = gram / count - col_mean[:, None] * row_mean[None, :]
    return covar * covar / (col_var[:, None] * row_var[None, :])


def column_stats(block):
    return (
        jnp.sum(block, axis=0, dtype=jnp.float32),
        jnp.sum(jnp.square(block.astype(jnp.float32)), axis=0),
    )


def pair_sums(columns, own_rows):
    return lax.dot_general(
        columns, own_rows, (((0,), (0,)), ((), ())), preferred_element_type=jnp.float32
    )


def shards(dosages):
    samples_here = dosages.shape[0]
    block_width = dosages.shape[1]
    shard_count = lax.axis_size("samp")
    count = jnp.float32(samples_here * shard_count)
    whole = lax.all_gather(dosages, "snp", axis=1, tiled=True)
    window_width = whole.shape[1]
    band = passed_along(whole[:, :OV], "win", -1)
    own_sum, own_sq = column_stats(dosages)
    total_sum, total_sq = lax.psum((own_sum, own_sq), "samp")
    win_sum, win_sq = (
        lax.all_gather(total_sum, "snp", axis=0, tiled=True),
        lax.all_gather(total_sq, "snp", axis=0, tiled=True),
    )
    next_sum, next_sq = passed_along((win_sum[:OV], win_sq[:OV]), "win", -1)
    win_cols = window_width // shard_count
    band_cols = OV // shard_count
    merged = jnp.concatenate(
        (
            whole.reshape(samples_here, shard_count, win_cols),
            band.reshape(samples_here, shard_count, band_cols),
        ),
        axis=2,
    ).reshape(samples_here, shard_count * (win_cols + band_cols))
    summed = lax.psum_scatter(pair_sums(merged, dosages), "samp", scatter_dimension=0, tiled=True)
    win_gram = summed[:win_cols]
    band_gram = summed[win_cols:]
    col_index = lax.axis_index("samp")
    row_index = lax.axis_index("snp")
    row_sum = lax.dynamic_slice_in_dim(win_sum, row_index * block_width, block_width, 0)
    row_sq = lax.dynamic_slice_in_dim(win_sq, row_index * block_width, block_width, 0)
    col_sum = lax.dynamic_slice_in_dim(win_sum, col_index * win_cols, win_cols, 0)
    col_sq = lax.dynamic_slice_in_dim(win_sq, col_index * win_cols, win_cols, 0)
    band_sum = lax.dynamic_slice_in_dim(next_sum, col_index * band_cols, band_cols, 0)
    band_sq = lax.dynamic_slice_in_dim(next_sq, col_index * band_cols, band_cols, 0)
    whole_out = squared_corr(win_gram, col_sum, col_sq, row_sum, row_sq, count)
    band_out = squared_corr(band_gram, band_sum, band_sq, row_sum, row_sq, count)
    return (whole_out[None], band_out[None])


def solution(mesh):
    return jax.shard_map(
        shards,
        mesh=mesh,
        in_specs=(P("samp", ("win", "snp")),),
        out_specs=(P("win", "samp", "snp"), P("win", "samp", "snp")),
        check_vma=False,
    )
```

profile of v0, /device:TPU:13, one launch (start us, length us, event | category | flops | bytes accessed | tf_op | source)
XLA Modules:
  0.0 416.1 jit_solution(9305339508099588703)
XLA Ops:
  7.2 0.0 all-gather.2.cloned.1.call-start
  7.2 0.7 all-gather.2.cloned.1.call-update
  7.9 0.0 reduce-scatter.2.cloned.1.call-start
  7.9 36.7 %all-gather.2.cloned.1.call-done = bf16[512,4096]{1,0:T(8,128)(2,1)} async-done(((bf16[512,1024]{1,0:T(8,128)(2,1)}), bf16[512,4096]{1,0:T(8,128)(2,1)}) %all-gather.2.cloned.1.call-update) | async-done | bytes 4194320 | tf_op jit(solution)/shard_map/all_gather | solution.py:44
  44.6 1.3 slice.20
  45.9 0.1 collective-permute-start
  46.0 4.4 %copy.3 = bf16[64,8,8,512]{3,2,1,0:T(8,128)(2,1)S(1)} copy(bf16[64,8,8,512]{3,1,2,0:T(8,128)(2,1)} %bitcast.14) | data formatting | bytes 8388608
  50.4 0.0 collective-permute-done
  50.4 0.3 copy.4
  50.7 0.5 pad_maximum_fusion
  51.2 0.0 copy-start
  51.2 1.2 copy.5
  52.4 0.0 copy-done
  52.4 9.9 %fusion.10 = f32[5120,1024]{1,0:T(8,128)} fusion(bf16[512,5120]{1,0:T(8,128)(2,1)S(1)} %bitcast.15, bf16[512,1024]{1,0:T(8,128)(2,1)S(1)} %copy-done), kind=kOutput, calls=%fused_computation.21 | convolution fusion | flops 5368709120 | bytes 27262976 | tf_op jit(solution)/shard_map/dot_general | solution.py:34
  62.3 0.0 reduce-scatter.2.cloned.1.call-update
  62.3 0.3 convert_reduce_fusion
  62.6 16.7 %all-reduce = (f32[1024]{0:T(1024)S(1)}, f32[1024]{0:T(1024)S(1)}) all-reduce(f32[1024]{0:T(1024)S(1)} %get-tuple-element.3, f32[1024]{0:T(1024)S(1)} %get-tuple-element.2), channel_id=1, replica_groups=mesh['samp'=8,'win'=1,'snp'=4] {'samp'}, use_global_device_ids=true, to_apply=%region_4.0 | all-reduce | flops 2048 | bytes 16384 | tf_op jit(solution)/shard_map/psum | solution.py:48
  79.4 8.2 %all_gather.10 = f32[4096]{0:T(1024)S(1)} all-gather(f32[1024]{0:T(1024)S(1)} %get-tuple-element.5), channel_id=1, replica_groups=mesh['samp'=8,'win'=1,'snp'=4] {'snp'}, dimensions={0}, use_global_device_ids=true | all-gather | bytes 20480 | tf_op jit(solution)/shard_map/all_gather | solution.py:50
  87.6 5.2 %all_gather.11 = f32[4096]{0:T(1024)S(1)} all-gather(f32[1024]{0:T(1024)S(1)} %get-tuple-element.4), channel_id=1, replica_groups=mesh['samp'=8,'win'=1,'snp'=4] {'snp'}, dimensions={0}, use_global_device_ids=true | all-gather | bytes 20480 | tf_op jit(solution)/shard_map/all_gather | solution.py:51
  92.8 0.1 dynamic-slice_multiply_fusion.1
  92.9 0.1 dynamic-slice_multiply_fusion.2
  93.0 310.8 %reduce-scatter.2.cloned.1.call-done = f32[640,1024]{1,0:T(8,128)} async-done(((f32[5120,1024]{1,0:T(8,128)}), f32[640,1024]{1,0:T(8,128)}) %reduce-scatter.2.cloned.1.call-update) | async-done | bytes 2621456 | tf_op jit(solution)/shard_map/reduce_scatter | solution.py:63
  403.7 3.5 fusion.4
  407.2 2.0 fusion.8
  (5 shorter events, 0.0 us)
Async XLA Ops:
  7.2 37.5 %all-gather.2.cloned.1.call-start = ((), (), s32[]{:S(2)}) async-start(), calls=%async_computation.1 | async-start | bytes 5242880 | tf_op jit(solution)/shard_map/all_gather | solution.py:44
  7.9 395.8 %reduce-scatter.2.cloned.1.call-start = ((), (), s32[]{:S(2)}) async-start(), calls=%async_computation.2 | async-start | bytes 23592960 | tf_op jit(solution)/shard_map/reduce_scatter | solution.py:63
  45.9 4.5 %collective-permute-start = (bf16[512,1024]{1,0:T(8,128)(2,1)S(1)}, bf16[512,1024]{1,0:T(8,128)(2,1)S(1)}, u32[]{:S(2)}, u32[]{:S(2)}) collective-permute-start(bf16[512,1024]{1,0:T(8,128)(2,1)S(1)} %slice.20), channel_id=1, source_target_pairs={{0,0},{1,1},{2,2},{3,3},{4,4},{5,5},{6,6},{7,7},{8,8},{9,9},{10,10... | collective-permute-start | bytes 3145736 | tf_op jit(solution)/shard_map/ppermute | solution.py:14
  51.2 1.2 copy-start
  92.8 0.1 collective-permute-start.1
  92.8 0.1 collective-permute-start.2
Sparse Core Ops, SparseCore 0:
  9.5 35.0 all-gather.1
  62.4 341.2 reduce-scatter.1
where the time goes:
time: 420 us; the launch traced here: 416 us
  waiting for transfers between devices  348 us (83%)
  blocking collectives  30.1 us (7%)
  between operations  14.1 us (3%)
  matrix products  9.9 us (2%)
  local copies, waits for them, and re-layouts  7.19 us (2%)
  other arithmetic  6.47 us (2%)
    reduce_scatter x1, waiting for transfers between devices, shards(): lax.psum_scatter(pair_sums(merged, dosages), 'samp', scatter_dimension=0,...  311 us
    all_gather x1, waiting for transfers between devices, shards(): whole = lax.all_gather(dosages, 'snp', axis=1, tiled=True)  36.7 us
    psum x1, blocking collectives, shards(): total_sum, total_sq = lax.psum((own_sum, own_sq), 'samp')  16.7 us
    dot_general x1, matrix products, pair_sums(): lax.dot_general(columns, own_rows, (((0,), (0,)), ((), ())), preferred_el...  9.9 us
  transfers between devices with their start and end apart: 5, of which 2 were waited for; matrix products, arithmetic and copies ran while one was open for 1% of the time, Pallas kernels for 0%

commit v1 on v0

v1 whole, which is shorter than its diff:
```python
import functools

import jax
import jax.numpy as jnp
from jax import lax
from jax.experimental import pallas as pl
from jax.experimental.pallas import tpu as pltpu
from jax.sharding import PartitionSpec as P

OV = 1024
VAR_FLOOR = 0.05
COLS = 2
PARTS = 2
MESH = pl.DeviceIdType.MESH


def plan(line):
    own = [(0, r, c) for r in range(line) for c in range(PARTS)]
    other = [(1, r, c) for r in range(line) for c in range(PARTS)]
    late = [v for v in other if v[1] in (1, 2) and v[2] == PARTS - 1]
    other = [v for v in other if v not in late] + late[::-1]
    lag = min(PARTS + 1, len(own))
    order = own[:lag]
    for k in range(lag, len(own)):
        order += [own[k], other[k - lag]]
    return order + other[len(own) - lag:]


def lookup(i, values):
    out = jnp.int32(0)
    for j, v in enumerate(values):
        if v:
            out = out + jnp.where(i == j, jnp.int32(v), jnp.int32(0))
    return out


def kernel(sizes, x_hbm, win_out, band_out, k_buf, j_buf, b_buf, k_stat, j_stat, b_stat,
           local_sem, k_recv, up_send, down_send, x_send, j_recv, j_send, b_recv, b_send, w_send, *band_wide):
    shard_count, windows, blocks, rows, width, jw, band, bw = sizes
    line = shard_count // COLS
    part_rows = rows // PARTS
    bits = blocks.bit_length() - 1
    chunks = shard_count * PARTS
    s = lax.axis_index("samp")
    n = lax.axis_index("snp")
    z = s // COLS
    x = s % COLS
    has_up = z < line - 1
    has_down = z > 0
    up = {"samp": jnp.minimum(s + COLS, shard_count - COLS + x)}
    down = {"samp": jnp.maximum(s - COLS, x)}
    across = {"samp": s + 1 - 2 * x}
    near = jnp.minimum(z, line - 1 - z)

    def bit(v, b):
        return (v // (1 << b)) % 2

    def flip(b):
        return {"snp": n + (1 << b) * (1 - 2 * bit(n, b))}

    j_home = (s * jw) // width
    j_off = pl.multiple_of((s * jw) % width, jw)
    b_home = (s * band) // width
    b_off = pl.multiple_of(((s * band) % width) // bw * bw, bw)
    j_rel = [(bit(n, b) + bit(j_home, b)) % 2 for b in range(bits)]
    b_rel = [(bit(n, b) + bit(b_home, b)) % 2 for b in range(bits)]

    def sends_on(rel, b):
        low = jnp.int32(0)
        for a in range(b + 1):
            low = low + rel[a]
        return low == 0

    def is_home(rel):
        total = jnp.int32(0)
        for r in rel:
            total = total + r
        return total == 0

    j_mine = is_home(j_rel)
    b_mine = is_home(b_rel)

    def k_copy(q, sem, to):
        return pltpu.make_async_remote_copy(
            src_ref=k_buf.at[q], dst_ref=k_buf.at[q], send_sem=sem.at[q], recv_sem=k_recv.at[q],
            device_id=to, device_id_type=MESH)

    def slice_copy(src, buf, q, send, recv, to):
        return pltpu.make_async_remote_copy(
            src_ref=src, dst_ref=buf.at[q], send_sem=send, recv_sem=recv.at[q],
            device_id=to, device_id_type=MESH)

    order = plan(line)
    band_sum = band_wide[0] if band_wide else band_out

    def item(o):
        side = lookup(o, [v[0] for v in order])
        r = lookup(o, [v[1] for v in order])
        c = lookup(o, [v[2] for v in order])
        odd = r % 2
        inner = z + jnp.where(odd == 1, 0 - (r + 1) // 2, r // 2)
        outer = jnp.where(z < line - 1 - z, r, line - 1 - r)
        zz = jnp.where(r <= 2 * near, inner, outer)
        xx = jnp.where(side == 1, 1 - x, x)
        return side, zz, c, (zz * COLS + xx) * PARTS + c

    def skips_x(zz, c):
        return (c == PARTS - 1) & ((zz == z + 1) | (zz == z - 1))

    for c in range(PARTS):
        pltpu.make_async_copy(x_hbm.at[pl.ds(c * part_rows, part_rows)],
                              k_buf.at[s * PARTS + c], local_sem.at[c]).start()

    barrier = pltpu.get_barrier_semaphore()

    def greet(to):
        pl.semaphore_signal(barrier, inc=1, device_id=to, device_id_type=MESH)

    pl.when(has_up)(lambda: greet(up))
    pl.when(has_down)(lambda: greet(down))
    greet(across)
    for b in range(bits):
        greet(flip(b))
    expected = 1 + bits
    if windows > 1:
        w = lax.axis_index("win")
        before = {"win": (w + windows - 1) % windows}
        after = {"win": (w + 1) % windows}
        greet(before)
        greet(after)
        expected += 2
    pl.semaphore_wait(barrier, expected + has_up.astype(jnp.int32) + has_down.astype(jnp.int32))

    k_stat[...] = jnp.zeros_like(k_stat)
    j_stat[...] = jnp.zeros_like(j_stat)
    b_stat[...] = jnp.zeros_like(b_stat)
    for c in range(PARTS):
        pltpu.make_async_copy(x_hbm.at[pl.ds(c * part_rows, part_rows)],
                              k_buf.at[s * PARTS + c], local_sem.at[c]).wait()

    last_own = max(i for i, v in enumerate(order) if v[0] == 0)
    cross_late = (s + 1 - 2 * x) * PARTS + PARTS - 1

    def take(o):
        side, zz, c, q = item(o)
        mine = (side == 0) & (zz == z)

        @pl.when(jnp.logical_not(mine))
        def _():
            k_copy(q, x_send, across).wait_recv()

        @pl.when((side == 0) & (zz <= z) & has_up)
        def _():
            k_copy(q, up_send, up).start()

        @pl.when((side == 0) & (zz >= z) & has_down)
        def _():
            k_copy(q, down_send, down).start()

        @pl.when((side == 0) & jnp.logical_not(skips_x(zz, c)))
        def _():
            k_copy(q, x_send, across).start()

        if line > 1:
            @pl.when((o == last_own) & has_up)
            def _():
                k_copy(cross_late, up_send, up).start()

            @pl.when((o == last_own) & has_down)
            def _():
                k_copy(cross_late, down_send, down).start()

        for b in reversed(range(bits)):
            @pl.when(j_mine)
            def _():
                slice_copy(k_buf.at[q, :, pl.ds(j_off, jw)], j_buf, q, j_send.at[b, q], j_recv, flip(b)).start()

            if windows == 1:
                @pl.when(b_mine)
                def _():
                    slice_copy(k_buf.at[q, :, pl.ds(b_off, bw)], b_buf, q, b_send.at[b, q], b_recv, flip(b)).start()
        if windows > 1:
            @pl.when(b_mine)
            def _():
                slice_copy(k_buf.at[q, :, pl.ds(b_off, bw)], b_buf, q, w_send.at[q], b_recv, before).start()

    def j_arrive(q):
        slice_copy(k_buf.at[q, :, pl.ds(j_off, jw)], j_buf, q, j_send.at[0, q], j_recv, flip(0)).wait_recv()

    def b_arrive(q):
        slice_copy(k_buf.at[q, :, pl.ds(b_off, bw)], b_buf, q, b_send.at[0, q], b_recv, flip(0)).wait_recv()

    def relay(o):
        _, _, _, q = item(o)

        @pl.when(jnp.logical_not(j_mine))
        def _():
            j_arrive(q)
            for b in reversed(range(bits)):
                @pl.when(sends_on(j_rel, b))
                def _():
                    slice_copy(j_buf.at[q], j_buf, q, j_send.at[b, q], j_recv, flip(b)).start()

        @pl.when(j_mine)
        def _():
            j_buf[q] = k_buf[q, :, pl.ds(j_off, jw)]

        def pass_band():
            b_arrive(q)
            for b in reversed(range(bits)):
                @pl.when(sends_on(b_rel, b))
                def _():
                    slice_copy(b_buf.at[q], b_buf, q, b_send.at[b, q], b_recv, flip(b)).start()

        if windows > 1:
            pass_band()
        else:
            pl.when(jnp.logical_not(b_mine))(pass_band)

            @pl.when(b_mine)
            def _():
                b_buf[q] = k_buf[q, :, pl.ds(b_off, bw)]

    def add_stats(stat, block):
        wide = block.astype(jnp.float32).reshape(part_rows // 8, 8, block.shape[-1])
        stat[0] += jnp.sum(wide, axis=0)
        stat[1] += jnp.sum(wide * wide, axis=0)

    def pair(a, b):
        return lax.dot_general(a, b, (((0,), (0,)), ((), ())), preferred_element_type=jnp.float32)

    def compute(o):
        _, _, _, q = item(o)
        whole = k_buf[q]
        j_cols = j_buf[q]
        b_cols = b_buf[q]
        add_stats(k_stat, whole)
        add_stats(j_stat, j_cols)
        add_stats(b_stat, b_cols)

        @pl.when(o == 0)
        def _():
            win_out[0] = pair(j_cols, whole)
            band_sum[0] = pair(b_cols, whole)

        @pl.when(o > 0)
        def _():
            win_out[0] += pair(j_cols, whole)
            band_sum[0] += pair(b_cols, whole)

    def step(o, carry):
        @pl.when(o < chunks)
        def _():
            take(o)

        @pl.when((o >= 1) & (o < chunks + 1))
        def _():
            relay(o - 1)

        @pl.when(o >= 2)
        def _():
            compute(o - 2)

        return carry

    lax.fori_loop(0, chunks + 2, step, 0)

    count = jnp.float32(rows * shard_count)

    def moments(total, square):
        mean = total / count
        return mean, 1.0 / jnp.maximum(square / count - mean * mean, VAR_FLOOR)

    row_mean, row_inv = moments(jnp.sum(k_stat[0], axis=0, keepdims=True), jnp.sum(k_stat[1], axis=0, keepdims=True))

    def finish(out, stat, height):
        mean, inv = moments(jnp.sum(stat[0].T, axis=1, keepdims=True), jnp.sum(stat[1].T, axis=1, keepdims=True))
        for a in range(0, height, 64):
            e = min(a + 64, height)
            covar = out[0, a:e] / count - mean[a:e] * row_mean
            out[0, a:e] = covar * covar * (inv[a:e] * row_inv)

    finish(win_out, j_stat, jw)
    finish(band_sum, b_stat, bw)
    if band_wide:
        band_out[0] = band_sum[0, pl.ds(pl.multiple_of((s * band) % bw, band), band)]

    def drain(o, carry):
        side, zz, c, q = item(o)

        @pl.when((side == 0) & (zz <= z) & has_up)
        def _():
            k_copy(q, up_send, up).wait_send()

        @pl.when((side == 0) & (zz >= z) & has_down)
        def _():
            k_copy(q, down_send, down).wait_send()

        @pl.when((side == 0) & jnp.logical_not(skips_x(zz, c)))
        def _():
            k_copy(q, x_send, across).wait_send()

        for b in range(bits):
            @pl.when(sends_on(j_rel, b))
            def _():
                slice_copy(j_buf.at[q], j_buf, q, j_send.at[b, q], j_recv, flip(b)).wait_send()

            @pl.when(sends_on(b_rel, b))
            def _():
                slice_copy(b_buf.at[q], b_buf, q, b_send.at[b, q], b_recv, flip(b)).wait_send()
        if windows > 1:
            @pl.when(b_mine)
            def _():
                slice_copy(b_buf.at[q], b_buf, q, w_send.at[q], b_recv, before).wait_send()
        return carry

    lax.fori_loop(0, chunks, drain, 0)
    if line > 1:
        @pl.when(has_up)
        def _():
            k_copy(cross_late, up_send, up).wait_send()

        @pl.when(has_down)
        def _():
            k_copy(cross_late, down_send, down).wait_send()


def shards(dosages):
    rows, width = dosages.shape
    shard_count = lax.axis_size("samp")
    windows = lax.axis_size("win")
    blocks = lax.axis_size("snp")
    jw = width * blocks // shard_count
    band = OV // shard_count
    bw = max(band, 128)
    bits = blocks.bit_length() - 1
    chunks = shard_count * PARTS
    part_rows = rows // PARTS
    sizes = (shard_count, windows, blocks, rows, width, jw, band, bw)
    dma = pltpu.SemaphoreType.DMA
    return pl.pallas_call(
        functools.partial(kernel, sizes),
        out_shape=(
            jax.ShapeDtypeStruct((1, jw, width), jnp.float32),
            jax.ShapeDtypeStruct((1, band, width), jnp.float32),
        ),
        in_specs=[pl.BlockSpec(memory_space=pl.ANY)],
        out_specs=[pl.BlockSpec(memory_space=pltpu.VMEM)] * 2,
        scratch_shapes=[
            pltpu.VMEM((chunks, part_rows, width), jnp.bfloat16),
            pltpu.VMEM((chunks, part_rows, jw), jnp.bfloat16),
            pltpu.VMEM((chunks, part_rows, bw), jnp.bfloat16),
            pltpu.VMEM((2, 8, width), jnp.float32),
            pltpu.VMEM((2, 8, jw), jnp.float32),
            pltpu.VMEM((2, 8, bw), jnp.float32),
            dma((PARTS,)),
            dma((chunks,)), dma((chunks,)), dma((chunks,)), dma((chunks,)),
            dma((chunks,)), dma((bits, chunks)),
            dma((chunks,)), dma((bits, chunks)), dma((chunks,)),
        ] + ([pltpu.VMEM((1, bw, width), jnp.float32)] if bw != band else []),
        compiler_params=pltpu.CompilerParams(
            collective_id=0, has_side_effects=True, vmem_limit_bytes=67043328
        ),
    )(dosages)


def solution(mesh):
    return jax.shard_map(
        shards,
        mesh=mesh,
        in_specs=(P("samp", ("win", "snp")),),
        out_specs=(P("win", "samp", "snp"), P("win", "samp", "snp")),
        check_vma=False,
    )
```

time: 420 us -> 113 us (0.27)
  the two profiles are of different devices: /device:TPU:13 before, /device:TPU:5 now
where the time goes in v1:
time: 113 us
  Pallas kernels  108 us (96%)
  local copies, waits for them, and re-layouts  4.01 us (4%)
    pallas_call x1, Pallas kernels, shards(): pl.pallas_call(functools.partial(kernel, sizes), out_shape=(jax.ShapeDtyp...  108 us
    unnamed x4, local copies, waits for them, and re-layouts  4.01 us

profile of v1, /device:TPU:5, one launch (start us, length us, event | category | flops | bytes accessed | tf_op | source)
XLA Modules:
  0.0 112.9 jit_solution(12416062752514688947)
XLA Ops:
  0.6 108.2 %shard_map.30 = (f32[1,512,1024]{2,1,0:T(8,128)}, f32[1,128,1024]{2,1,0:T(8,128)}) custom-call(bf16[512,1024]{1,0:T(8,128)(2,1)} %x_hbm.1), custom_call_target="tpu_custom_call" | custom-call | tf_op jit(solution)/shard_map/pallas_call | solution.py:341
  108.8 0.0 copy-start
  108.9 3.2 %copy.5 = f32[1,512,1024]{2,1,0:T(8,128)} copy(f32[1,512,1024]{2,1,0:T(8,128)} %get-tuple-element.4) | data formatting | bytes 4194304
  112.1 0.0 copy-done
  112.1 0.8 copy.6
Async XLA Ops:
  108.8 3.2 %copy-start = (f32[1,128,1024]{2,1,0:T(8,128)S(1)}, f32[1,128,1024]{2,1,0:T(8,128)}, u32[]{:S(2)}) copy-start(f32[1,128,1024]{2,1,0:T(8,128)} %get-tuple-element.5) | copy-start | bytes 1572868

commit v2 on v1

--- a/solution.py
+++ b/solution.py
@@ -10,15 +10,17 @@
 OV = 1024
 VAR_FLOOR = 0.05
 COLS = 2
-PARTS = 2
+PARTS = 4
+LATE = PARTS // 2
 MESH = pl.DeviceIdType.MESH
 
 
 def plan(line):
     own = [(0, r, c) for r in range(line) for c in range(PARTS)]
     other = [(1, r, c) for r in range(line) for c in range(PARTS)]
-    late = [v for v in other if v[1] in (1, 2) and v[2] == PARTS - 1]
-    other = [v for v in other if v not in late] + late[::-1]
+    late = [v for v in other if v[1] in (1, 2) and v[2] >= LATE]
+    other = [v for v in other if v not in late]
+    other = other[:-1] + [v for v in late if v[1] == 2] + other[-1:] + [v for v in late if v[1] == 1]
     lag = min(PARTS + 1, len(own))
     order = own[:lag]
     for k in range(lag, len(own)):
@@ -105,7 +107,7 @@
         return side, zz, c, (zz * COLS + xx) * PARTS + c
 
     def skips_x(zz, c):
-        return (c == PARTS - 1) & ((zz == z + 1) | (zz == z - 1))
+        return (c >= LATE) & ((zz == z + 1) | (zz == z - 1))
 
     for c in range(PARTS):
         pltpu.make_async_copy(x_hbm.at[pl.ds(c * part_rows, part_rows)],
@@ -139,7 +141,7 @@
                               k_buf.at[s * PARTS + c], local_sem.at[c]).wait()
 
     last_own = max(i for i, v in enumerate(order) if v[0] == 0)
-    cross_late = (s + 1 - 2 * x) * PARTS + PARTS - 1
+    cross_late = [(s + 1 - 2 * x) * PARTS + c for c in range(LATE, PARTS)]
 
     def take(o):
         side, zz, c, q = item(o)
@@ -164,11 +166,13 @@
         if line > 1:
             @pl.when((o == last_own) & has_up)
             def _():
-                k_copy(cross_late, up_send, up).start()
+                for late in cross_late:
+                    k_copy(late, up_send, up).start()
 
             @pl.when((o == last_own) & has_down)
             def _():
-                k_copy(cross_late, down_send, down).start()
+                for late in cross_late:
+                    k_copy(late, down_send, down).start()
 
         for b in reversed(range(bits)):
             @pl.when(j_mine)
@@ -253,17 +257,17 @@
         def _():
             take(o)
 
-        @pl.when((o >= 1) & (o < chunks + 1))
-        def _():
-            relay(o - 1)
-
-        @pl.when(o >= 2)
-        def _():
-            compute(o - 2)
+        @pl.when((o >= 2) & (o < chunks + 2))
+        def _():
+            relay(o - 2)
+
+        @pl.when(o >= 3)
+        def _():
+            compute(o - 3)
 
         return carry
 
-    lax.fori_loop(0, chunks + 2, step, 0)
+    lax.fori_loop(0, chunks + 3, step, 0)
 
     count = jnp.float32(rows * shard_count)
 
@@ -318,11 +322,13 @@
     if line > 1:
         @pl.when(has_up)
         def _():
-            k_copy(cross_late, up_send, up).wait_send()
+            for late in cross_late:
+                k_copy(late, up_send, up).wait_send()
 
         @pl.when(has_down)
         def _():
-            k_copy(cross_late, down_send, down).wait_send()
+            for late in cross_late:
+                k_copy(late, down_send, down).wait_send()
 
 
 def shards(dosages):

time: 113 us -> 115 us (1.018)
  the two profiles are of different devices: /device:TPU:5 before, /device:TPU:13 now
where the time goes in v2:
time: 115 us
  Pallas kernels  110 us (96%)
  local copies, waits for them, and re-layouts  4.01 us (3%)
    pallas_call x1, Pallas kernels, shards(): pl.pallas_call(functools.partial(kernel, sizes), out_shape=(jax.ShapeDtyp...  110 us
    unnamed x4, local copies, waits for them, and re-layouts  4.01 us

profile of v2, /device:TPU:13, one launch (start us, length us, event | category | flops | bytes accessed | tf_op | source)
XLA Modules:
  0.0 114.7 jit_solution(11645797991578503943)
XLA Ops:
  0.6 110.1 %shard_map.30 = (f32[1,512,1024]{2,1,0:T(8,128)}, f32[1,128,1024]{2,1,0:T(8,128)}) custom-call(bf16[512,1024]{1,0:T(8,128)(2,1)} %x_hbm.1), custom_call_target="tpu_custom_call" | custom-call | tf_op jit(solution)/shard_map/pallas_call | solution.py:347
  110.7 0.0 copy-start
  110.7 3.2 %copy.5 = f32[1,512,1024]{2,1,0:T(8,128)} copy(f32[1,512,1024]{2,1,0:T(8,128)} %get-tuple-element.4) | data formatting | bytes 4194304
  113.9 0.0 copy-done
  113.9 0.8 copy.6
Async XLA Ops:
  110.7 3.2 %copy-start = (f32[1,128,1024]{2,1,0:T(8,128)S(1)}, f32[1,128,1024]{2,1,0:T(8,128)}, u32[]{:S(2)}) copy-start(f32[1,128,1024]{2,1,0:T(8,128)} %get-tuple-element.5) | copy-start | bytes 1572868

commit v3 on v1

--- a/solution.py
+++ b/solution.py
@@ -253,17 +253,17 @@
         def _():
             take(o)
 
-        @pl.when((o >= 1) & (o < chunks + 1))
-        def _():
-            relay(o - 1)
-
-        @pl.when(o >= 2)
-        def _():
-            compute(o - 2)
+        @pl.when((o >= 2) & (o < chunks + 2))
+        def _():
+            relay(o - 2)
+
+        @pl.when(o >= 3)
+        def _():
+            compute(o - 3)
 
         return carry
 
-    lax.fori_loop(0, chunks + 2, step, 0)
+    lax.fori_loop(0, chunks + 3, step, 0)
 
     count = jnp.float32(rows * shard_count)
 

time: 113 us -> 111 us (0.982)
  the two profiles are of different devices: /device:TPU:5 before, /device:TPU:13 now
where the time goes in v3:
time: 111 us; the launch traced here: 109 us
  Pallas kernels  105 us (95%)
  local copies, waits for them, and re-layouts  4.01 us (4%)
    pallas_call x1, Pallas kernels, shards(): pl.pallas_call(functools.partial(kernel, sizes), out_shape=(jax.ShapeDtyp...  105 us
    unnamed x4, local copies, waits for them, and re-layouts  4.01 us

profile of v3, /device:TPU:13, one launch (start us, length us, event | category | flops | bytes accessed | tf_op | source)
XLA Modules:
  0.0 109.2 jit_solution(6581634844757819537)
XLA Ops:
  0.6 104.6 %shard_map.30 = (f32[1,512,1024]{2,1,0:T(8,128)}, f32[1,128,1024]{2,1,0:T(8,128)}) custom-call(bf16[512,1024]{1,0:T(8,128)(2,1)} %x_hbm.1), custom_call_target="tpu_custom_call" | custom-call | tf_op jit(solution)/shard_map/pallas_call | solution.py:341
  105.2 0.0 copy-start
  105.2 3.2 %copy.5 = f32[1,512,1024]{2,1,0:T(8,128)} copy(f32[1,512,1024]{2,1,0:T(8,128)} %get-tuple-element.4) | data formatting | bytes 4194304
  108.4 0.0 copy-done
  108.4 0.8 copy.6
Async XLA Ops:
  105.2 3.2 %copy-start = (f32[1,128,1024]{2,1,0:T(8,128)S(1)}, f32[1,128,1024]{2,1,0:T(8,128)}, u32[]{:S(2)}) copy-start(f32[1,128,1024]{2,1,0:T(8,128)} %get-tuple-element.5) | copy-start | bytes 1572868

commit v4 on v3

--- a/solution.py
+++ b/solution.py
@@ -18,7 +18,8 @@
     own = [(0, r, c) for r in range(line) for c in range(PARTS)]
     other = [(1, r, c) for r in range(line) for c in range(PARTS)]
     late = [v for v in other if v[1] in (1, 2) and v[2] == PARTS - 1]
-    other = [v for v in other if v not in late] + late[::-1]
+    other = [v for v in other if v not in late]
+    other = other[:-1] + [v for v in late if v[1] == 2] + other[-1:] + [v for v in late if v[1] == 1]
     lag = min(PARTS + 1, len(own))
     order = own[:lag]
     for k in range(lag, len(own)):

time: 111 us -> 109 us (0.982); the launches traced: 109 us -> 109 us
  no operation moved by 1% of the time
where the time goes in v4:
time: 109 us
  Pallas kernels  105 us (96%)
  local copies, waits for them, and re-layouts  4.01 us (4%)
    pallas_call x1, Pallas kernels, shards(): pl.pallas_call(functools.partial(kernel, sizes), out_shape=(jax.ShapeDtyp...  105 us
    unnamed x4, local copies, waits for them, and re-layouts  4.01 us

profile of v4, /device:TPU:13, one launch (start us, length us, event | category | flops | bytes accessed | tf_op | source)
XLA Modules:
  0.0 109.2 jit_solution(10130384724290694615)
XLA Ops:
  0.6 104.6 %shard_map.30 = (f32[1,512,1024]{2,1,0:T(8,128)}, f32[1,128,1024]{2,1,0:T(8,128)}) custom-call(bf16[512,1024]{1,0:T(8,128)(2,1)} %x_hbm.1), custom_call_target="tpu_custom_call" | custom-call | tf_op jit(solution)/shard_map/pallas_call | solution.py:342
  105.2 0.0 copy-start
  105.2 3.2 %copy.5 = f32[1,512,1024]{2,1,0:T(8,128)} copy(f32[1,512,1024]{2,1,0:T(8,128)} %get-tuple-element.4) | data formatting | bytes 4194304
  108.4 0.0 copy-done
  108.4 0.8 copy.6
Async XLA Ops:
  105.2 3.2 %copy-start = (f32[1,128,1024]{2,1,0:T(8,128)S(1)}, f32[1,128,1024]{2,1,0:T(8,128)}, u32[]{:S(2)}) copy-start(f32[1,128,1024]{2,1,0:T(8,128)} %get-tuple-element.5) | copy-start | bytes 1572868

commit v5 on v4

--- a/solution.py
+++ b/solution.py
@@ -254,17 +254,17 @@
         def _():
             take(o)
 
-        @pl.when((o >= 2) & (o < chunks + 2))
-        def _():
-            relay(o - 2)
-
-        @pl.when(o >= 3)
-        def _():
-            compute(o - 3)
+        @pl.when((o >= 3) & (o < chunks + 3))
+        def _():
+            relay(o - 3)
+
+        @pl.when(o >= 4)
+        def _():
+            compute(o - 4)
 
         return carry
 
-    lax.fori_loop(0, chunks + 3, step, 0)
+    lax.fori_loop(0, chunks + 4, step, 0)
 
     count = jnp.float32(rows * shard_count)
 

time: 109 us -> 112 us (1.028)
  Pallas kernels: 105 us -> 107 us
    pallas_call x1, Pallas kernels: 105 us -> 107 us  [shards(): pl.pallas_call(functools.partial(kernel, sizes), out_shape=(jax.ShapeDtyp...]
where the time goes in v5:
time: 112 us; the launch traced here: 111 us
  Pallas kernels  107 us (96%)
  local copies, waits for them, and re-layouts  4.01 us (4%)
    pallas_call x1, Pallas kernels, shards(): pl.pallas_call(functools.partial(kernel, sizes), out_shape=(jax.ShapeDtyp...  107 us
    unnamed x4, local copies, waits for them, and re-layouts  4.01 us

profile of v5, /device:TPU:13, one launch (start us, length us, event | category | flops | bytes accessed | tf_op | source)
XLA Modules:
  0.0 111.4 jit_solution(8194593018341044717)
XLA Ops:
  0.6 106.7 %shard_map.30 = (f32[1,512,1024]{2,1,0:T(8,128)}, f32[1,128,1024]{2,1,0:T(8,128)}) custom-call(bf16[512,1024]{1,0:T(8,128)(2,1)} %x_hbm.1), custom_call_target="tpu_custom_call" | custom-call | tf_op jit(solution)/shard_map/pallas_call | solution.py:342
  107.4 0.0 copy-start
  107.4 3.2 %copy.5 = f32[1,512,1024]{2,1,0:T(8,128)} copy(f32[1,512,1024]{2,1,0:T(8,128)} %get-tuple-element.4) | data formatting | bytes 4194304
  110.6 0.0 copy-done
  110.6 0.8 copy.6
Async XLA Ops:
  107.4 3.2 %copy-start = (f32[1,128,1024]{2,1,0:T(8,128)S(1)}, f32[1,128,1024]{2,1,0:T(8,128)}, u32[]{:S(2)}) copy-start(f32[1,128,1024]{2,1,0:T(8,128)} %get-tuple-element.5) | copy-start | bytes 1572868
